TPU v7x, 256 devices: a whole 4x4x8 slice. The times are simulated.
256 devices in a mesh: coarse: 4 (over y), fine: 8 (over z), group: 8 (over x, core).
Axes of the slice: x: 4, y: 4, z: 8, core: 2. Of those that a mesh axis runs over, the one named last changes fastest.
Arguments:
- fresh_keys: bfloat16 [32, 16384, 8, 128], P(None, ('coarse', 'fine'), 'group'), may hold values from -6 to 6
- fresh_values: bfloat16 [32, 16384, 8, 128], P(None, ('coarse', 'fine'), 'group'), may hold values from -6 to 6
- turn_angle: float32 [16384, 64], replicated, may hold values from -3.140625 to 3.140625
- key_gain: float32 [128], replicated, may hold values from 0.25 to 1.75
Outputs:
- decode_keys: bfloat16 [32, 8, 128, 16384], P(('coarse', 'fine'), 'group')
- decode_values: bfloat16 [32, 16384, 8, 128], P(('coarse', 'fine'), None, 'group')
- key_scale: float32 [32, 8, 128], P(('coarse', 'fine'), 'group')
All inputs are finite; a program needn't handle non-finite values. Where the computation divides by a largest or mean magnitude, that divisor is 1e-20 or more.
Results may differ from a plain program's by a relative error of at most 0.001.
Values may be sent and summed in bfloat16 or wider, within the bound.
A program may use at most 128 MiB of HBM per device.

v0:
```python
import jax
import jax.numpy as jnp
from jax import lax
from jax.sharding import PartitionSpec as P


def turn_pairs(vectors, angle):
    half = vectors.shape[-1] // 2
    cosine, sine = (jnp.cos(angle)[None, :, None, :], jnp.sin(angle)[None, :, None, :])
    first, second = (vectors[..., :half], vectors[..., half:])
    return jnp.concatenate(
        [first * cosine - second * sine, second * cosine + first * sine], axis=-1
    )


def root_norm(vectors, row_gain):
    return (
        vectors * lax.rsqrt(jnp.mean(vectors * vectors, axis=-1, keepdims=True) + 1e-06) * row_gain
    )


def ready_to_store(plain_keys, angle, key_gain):
    wide_keys = plain_keys.astype(jnp.float32)
    wide_keys = root_norm(wide_keys, key_gain)
    return turn_pairs(wide_keys, angle)


def local(fresh_keys, fresh_values, turn_angle, key_gain):
    moved_keys, decode_values = (
        lax.all_to_all(fresh_keys, ("coarse", "fine"), split_axis=0, concat_axis=1, tiled=True),
        lax.all_to_all(fresh_values, ("coarse", "fine"), split_axis=0, concat_axis=1, tiled=True),
    )
    turned_keys = ready_to_store(moved_keys, turn_angle, key_gain)
    key_scale = jnp.max(jnp.abs(turned_keys), axis=1)
    narrow_keys = (turned_keys / key_scale[:, None]).astype(jnp.bfloat16)
    decode_keys = jnp.transpose(narrow_keys, (0, 2, 3, 1))
    return (decode_keys, decode_values, key_scale)


def solution(mesh):
    in_specs = (
        P(None, ("coarse", "fine"), "group", None),
        P(None, ("coarse", "fine"), "group", None),
        P(),
        P(),
    )
    out_specs = (
        P(("coarse", "fine"), "group", None, None),
        P(("coarse", "fine"), None, "group", None),
        P(("coarse", "fine"), "group", None),
    )
    return jax.shard_map(local, mesh=mesh, in_specs=in_specs, out_specs=out_specs, check_vma=False)
```

profile of v0, /device:TPU:2, one launch (start us, length us, event | category | flops | bytes accessed | tf_op | source)
XLA Modules:
  0.0 215.1 jit_solution(550295170954146502)
XLA Ops:
  0.6 11.6 %all-to-all-start = ((bf16[32,512,1,128]{3,1,2,0:T(8,128)(2,1)}), bf16[32,512,1,128]{3,1,2,0:T(8,128)(2,1)}, u32[]{:S(2)}, u32[]{:S(2)}) async-start(bf16[32,512,1,128]{3,1,2,0:T(8,128)(2,1)} %param.4), calls=%async_computation | async-start | bytes 8388608 | tf_op jit(solution)/shard_map/all_to_all | solution.py:30
  12.3 16.7 %fusion.3 = (f32[16384,64]{0,1:T(8,128)}, f32[16384,64]{0,1:T(8,128)}) fusion(f32[16384,64]{0,1:T(8,128)} %param.6), kind=kLoop, calls=%fused_computation.13 | loop fusion | bytes 12582912 | tf_op jit(solution)/shard_map/cos | solution.py:9
  28.9 80.3 %all-to-all-done = bf16[32,512,1,128]{3,1,2,0:T(8,128)(2,1)} async-done(((bf16[32,512,1,128]{3,1,2,0:T(8,128)(2,1)}), bf16[32,512,1,128]{3,1,2,0:T(8,128)(2,1)}, u32[]{:S(2)}, u32[]{:S(2)}) %all-to-all-start) | async-done | bytes 4194336 | tf_op jit(solution)/shard_map/all_to_all | solution.py:30
  109.3 5.1 %all-to-all-start.1 = ((bf16[32,512,1,128]{3,1,2,0:T(8,128)(2,1)}), bf16[32,512,1,128]{3,1,2,0:T(8,128)(2,1)}, u32[]{:S(2)}, u32[]{:S(2)}) async-start(bf16[32,512,1,128]{3,1,2,0:T(8,128)(2,1)} %param.5), calls=%async_computation.1 | async-start | bytes 8388608 | tf_op jit(solution)/shard_map/all_to_all | solution.py:31
  114.4 7.0 %copy.8 = f32[1,16384,1,128]{1,3,2,0:T(8,128)} copy(bf16[1,16384,1,128]{3,1,2,0:T(8,128)(2,1)} %bitcast.22) | data formatting | bytes 12582912 | tf_op jit(solution)/shard_map/convert_element_type | solution.py:23
  121.3 0.0 copy-start.2
  121.3 4.4 %multiply_reduce_fusion = f32[32,512]{1,0:T(8,128)S(1)} fusion(bf16[32,512,1,128]{3,1,2,0:T(8,128)(2,1)} %all-to-all-done), kind=kLoop, calls=%fused_computation.4 | loop fusion | flops 6275072 | bytes 4259840 | tf_op jit(solution)/shard_map/reduce_sum | solution.py:18
  125.8 0.0 copy-done.2
  125.9 7.6 %multiply_multiply_fusion = f32[1,16384,1,128]{1,3,2,0:T(8,128)} fusion(f32[1,16384,1,128]{1,3,2,0:T(8,128)} %copy.8, f32[128]{0:T(128)S(1)} %copy-done.2, f32[16384]{0:T(1024)S(1)} %bitcast.23), kind=kLoop, calls=%fused_computation.3 | loop fusion | flops 4194304 | bytes 16843264 | tf_op jit(solution)/shard_map/mul | solution.py:18
  133.4 8.8 %fusion = (f32[1,16384,1,64]{1,3,2,0:T(8,128)S(1)}, f32[1,16384,1,64]{1,3,2,0:T(8,128)}) fusion(f32[16384,64]{0,1:T(8,128)} %get-tuple-element.6, f32[16384,64]{0,1:T(8,128)} %get-tuple-element.5, f32[1,16384,1,128]{1,3,2,0:T(8,128)} %multiply_multiply_fusion), kind=kLoop, calls=%fused_computation.7 | loop fusion | flops 6291456 | bytes 25165824 | tf_op jit(solution)/shard_map/sub | solution.py:12
  142.2 0.0 copy-start
  142.2 3.1 %abs_reduce_fusion = f32[128]{0:T(128)S(1)} fusion(f32[1,16384,1,64]{1,3,2,0:T(8,128)} %get-tuple-element.4, f32[1,16384,1,64]{1,3,2,0:T(8,128)S(1)} %get-tuple-element.3), kind=kLoop, calls=%fused_computation.2 | loop fusion | flops 6291328 | bytes 8389120 | tf_op jit(solution)/shard_map/reduce_max | solution.py:34
  145.3 0.3 copy-done
  145.6 0.0 copy-start.1
  145.6 2.5 %fusion.2 = bf16[1,1,128,16384]{3,2,1,0:T(8,128)(2,1)} fusion(f32[128]{0:T(128)S(1)} %abs_reduce_fusion, f32[1,16384,1,64]{1,3,2,0:T(8,128)S(1)} %copy-done, f32[1,16384,1,64]{1,3,2,0:T(8,128)S(1)} %get-tuple-element.3), kind=kLoop, calls=%fused_computation.11 | loop fusion | flops 6291456 | bytes 12583424 | tf_op jit(solution)/shard_map/transpose | solution.py:36
  148.2 0.0 copy-done.1
  148.2 63.2 %all-to-all-done.1 = bf16[32,512,1,128]{3,1,2,0:T(8,128)(2,1)} async-done(((bf16[32,512,1,128]{3,1,2,0:T(8,128)(2,1)}), bf16[32,512,1,128]{3,1,2,0:T(8,128)(2,1)}, u32[]{:S(2)}, u32[]{:S(2)}) %all-to-all-start.1) | async-done | bytes 4194336 | tf_op jit(solution)/shard_map/all_to_all | solution.py:31
  211.3 3.7 %copy.11 = bf16[1,16384,1,128]{3,1,2,0:T(8,128)(2,1)} copy(bf16[1,16384,1,128]{3,1,2,0:T(8,128)(2,1)} %bitcast.4) | data formatting | bytes 8388608
  (2 shorter events, 0.0 us)
Async XLA Ops:
  0.6 108.6 %all-to-all-start = ((bf16[32,512,1,128]{3,1,2,0:T(8,128)(2,1)}), bf16[32,512,1,128]{3,1,2,0:T(8,128)(2,1)}, u32[]{:S(2)}, u32[]{:S(2)}) async-start(bf16[32,512,1,128]{3,1,2,0:T(8,128)(2,1)} %param.4), calls=%async_computation | async-start | bytes 8388608 | tf_op jit(solution)/shard_map/all_to_all | solution.py:30
  109.3 102.1 %all-to-all-start.1 = ((bf16[32,512,1,128]{3,1,2,0:T(8,128)(2,1)}), bf16[32,512,1,128]{3,1,2,0:T(8,128)(2,1)}, u32[]{:S(2)}, u32[]{:S(2)}) async-start(bf16[32,512,1,128]{3,1,2,0:T(8,128)(2,1)} %param.5), calls=%async_computation.1 | async-start | bytes 8388608 | tf_op jit(solution)/shard_map/all_to_all | solution.py:31
  121.3 4.5 %copy-start.2 = (f32[128]{0:T(128)S(1)}, f32[128]{0:T(128)}, u32[]{:S(2)}) copy-start(f32[128]{0:T(128)} %param.7) | copy-start | bytes 1540
  142.2 3.4 %copy-start = (f32[1,16384,1,64]{1,3,2,0:T(8,128)S(1)}, f32[1,16384,1,64]{1,3,2,0:T(8,128)}, u32[]{:S(2)}) copy-start(f32[1,16384,1,64]{1,3,2,0:T(8,128)} %get-tuple-element.4) | copy-start | bytes 12582916
  145.6 2.5 %copy-start.1 = (f32[128]{0:T(128)}, f32[128]{0:T(128)S(1)}, u32[]{:S(2)}) copy-start(f32[128]{0:T(128)S(1)} %abs_reduce_fusion) | copy-start | bytes 1540
where the time goes:
time: 215 us
  waiting for transfers between devices  144 us (67%)
  local copies, waits for them, and re-layouts  27.7 us (13%)
  other arithmetic  26.4 us (12%)
  starting transfers between devices  16.7 us (8%)
    all_to_all x1, waiting for transfers between devices, local(): lax.all_to_all(fresh_keys, ('coarse', 'fine'), split_axis=0, concat_axis=...  80.3 us
    all_to_all x1, waiting for transfers between devices, local(): lax.all_to_all(fresh_values, ('coarse', 'fine'), split_axis=0, concat_axi...  63.2 us
    cos x1, local copies, waits for them, and re-layouts, turn_pairs(): jnp.cos(angle)[None, :, None, :]  16.7 us
    all_to_all x1, starting transfers between devices, local(): lax.all_to_all(fresh_keys, ('coarse', 'fine'), split_axis=0, concat_axis=...  11.6 us
    sub x1, other arithmetic, turn_pairs(): first * cosine - second * sine  8.79 us
    mul x1, other arithmetic, root_norm(): vectors * lax.rsqrt(jnp.mean(vectors * vectors, axis=-1, keepdims=True) +...  7.55 us
    convert_element_type x1, local copies, waits for them, and re-layouts, ready_to_store(): wide_keys = plain_keys.astype(jnp.float32)  6.98 us
    all_to_all x1, starting transfers between devices, local(): lax.all_to_all(fresh_values, ('coarse', 'fine'), split_axis=0, concat_axi...  5.09 us
  transfers between devices with their start and end apart: 2, of which 2 were waited for; matrix products, arithmetic and copies ran while one was open for 23% of the time, Pallas kernels for 0%

commit v1 on v0

v1 whole, which is shorter than its diff:
```python
import jax
import jax.numpy as jnp
from jax import lax
from jax.experimental import pallas as pl
from jax.experimental.pallas import tpu as pltpu
from jax.sharding import PartitionSpec as P

MESH = pl.DeviceIdType.MESH
COARSE, FINE = 4, 8
PARTS = COARSE * FINE
CHUNK = 128
KEYS, VALUES = 0, 1
LAG = 3
AHEAD = 4
OFFSETS = (4, 3, -3, 2, -2, 1, -1, 0)
FORWARD4 = ((0, 2), (1, 3))


def coarse_plan():
    plan = []
    for array in (KEYS, VALUES):
        plan += [[(array, 1, o), (array, 3, o)] for o in OFFSETS]
        plan += [[(array, 2, o)] for o in OFFSETS]
    return plan


def fine_plan(way):
    ready = {e: j + LAG + (e[1] == 2) for j, step in enumerate(coarse_plan()) for e in step}
    waiting = []
    for array in (KEYS, VALUES):
        for rows in range(COARSE):
            for hops in range(1, FINE // 2 + 1):
                if hops == FINE // 2 and (rows in FORWARD4[array]) != (way == 1):
                    continue
                off = hops if hops == FINE // 2 else way * hops
                waiting.append((ready.get((array, rows, off), 0), array, hops, rows, 0))
    plan = []
    while waiting:
        now = len(plan)
        best = min(
            (w for w in waiting if w[0] <= now), key=lambda w: (w[1], w[4] - w[2], w[0], w[3])
        )
        waiting.remove(best)
        plan.append(best[1:])
        _, array, hops, rows, done = best
        if done + 1 < hops:
            waiting.append((now + LAG, array, hops, rows, done + 1))
    return plan


COARSE_PLAN = coarse_plan()
FINE_PLAN = {way: fine_plan(way) for way in (1, -1)}
STEPS = len(FINE_PLAN[1])
SLOT = {}
for _step in COARSE_PLAN:
    for _array, _rows, _off in _step:
        if _off:
            SLOT["staged", _array, _rows, _off] = len(SLOT)
for _way in FINE_PLAN:
    for _array, _hops, _rows, _done in FINE_PLAN[_way]:
        if _done:
            SLOT["passing", _way, _array, _hops, _rows, _done] = len(SLOT)
SLOTS = len(SLOT)
FIRST_TURN = STEPS // 2 + LAG + 1
TURNS = 2
FIRST_NARROW = FIRST_TURN + PARTS // TURNS
NARROWS = 4


def kernel(keys, values, angle, gain, out_keys, out_values, out_scale,
           held, turned, angles, peak, gains, box,
           sent, box_came, key_came, value_came, local_sem):
    c, f, g = (lax.axis_index(name) for name in ("coarse", "fine", "group"))
    block = held.shape[1]
    me = c * FINE + f
    source_of = (keys, values)
    final_of = (held, out_values)

    def at(row, column):
        return ((c + row) % COARSE, (f + column + FINE) % FINE, g)

    near = [(0, 1), (0, -1), (1, 0), (3, 0), (2, 0)]
    barrier = pltpu.get_barrier_semaphore()
    for row, column in near:
        pl.semaphore_signal(barrier, inc=1, device_id=at(row, column), device_id_type=MESH)
    pl.semaphore_wait(barrier, len(near))

    def came(array, device):
        return key_came.at[device] if array == KEYS else value_came

    def send_coarse(array, rows, off):
        there = at(rows, 0)
        if off:
            slot = SLOT["staged", array, rows, off]
            target, arrived = box.at[slot], box_came.at[slot]
        else:
            target, arrived = final_of[array].at[me], came(array, me)
        pltpu.make_async_remote_copy(
            src_ref=source_of[array].at[there[0] * FINE + (f + off + FINE) % FINE],
            dst_ref=target, send_sem=sent, recv_sem=arrived, device_id=there, device_id_type=MESH,
        ).start()

    def send_fine(way, array, hops, rows, done):
        off = hops if hops == FINE // 2 else way * hops
        if done:
            slot = SLOT["passing", way, array, hops, rows, done]
        elif rows:
            slot = SLOT["staged", array, rows, off]
        else:
            slot = None
        if slot is None:
            source = source_of[array].at[c * FINE + (f + off + FINE) % FINE]
        else:
            source = box.at[slot]
            pltpu.make_async_copy(source, source, box_came.at[slot]).wait()
        if done + 1 < hops:
            slot = SLOT["passing", way, array, hops, rows, done + 1]
            target, arrived = box.at[slot], box_came.at[slot]
        else:
            home = ((c + COARSE - rows) % COARSE) * FINE + (f - way * done + FINE) % FINE
            target, arrived = final_of[array].at[home], came(array, home)
        pltpu.make_async_remote_copy(
            src_ref=source, dst_ref=target, send_sem=sent, recv_sem=arrived,
            device_id=at(0, way), device_id_type=MESH,
        ).start()

    def exchange(step):
        if step + AHEAD < len(COARSE_PLAN):
            for entry in COARSE_PLAN[step + AHEAD]:
                send_coarse(*entry)
        for way in FINE_PLAN:
            send_fine(way, *FINE_PLAN[way][step])

    def turn(source):
        @pl.loop(0, block // CHUNK)
        def _(n):
            plain = held[source, pl.ds(pl.multiple_of(n * CHUNK, CHUNK), CHUNK), :]
            wide = plain.astype(jnp.float32).T
            mean = jnp.sum(wide * wide, axis=0, keepdims=True) * (1.0 / wide.shape[0])
            wide = wide * lax.rsqrt(mean + 1e-06) * gains[...]
            where = pl.ds(pl.multiple_of(source * block + n * CHUNK, CHUNK), CHUNK)
            a = angles[:, where]
            cosine, sine = jnp.cos(a), jnp.sin(a)
            half = a.shape[0]
            first, second = wide[:half], wide[half:]
            low = first * cosine - second * sine
            high = second * cosine + first * sine
            turned[:half, where] = low
            turned[half:, where] = high
            peak[:half] = jnp.maximum(peak[:half], jnp.abs(low))
            peak[half:] = jnp.maximum(peak[half:], jnp.abs(high))

    def narrow(i):
        where = pl.ds(pl.multiple_of(i * block, block), block)
        scale = jnp.max(peak[...], axis=1, keepdims=True)
        out_keys[:, where] = (turned[:, where] / scale).astype(out_keys.dtype)

    for entry in sum(COARSE_PLAN[:AHEAD], []):
        send_coarse(*entry)
    own_keys = pltpu.make_async_copy(keys.at[me], held.at[me], local_sem.at[0])
    own_values = pltpu.make_async_copy(values.at[me], out_values.at[me], local_sem.at[1])
    get_angles = pltpu.make_async_copy(angle, angles, local_sem.at[2])
    for step in range(FIRST_TURN):
        exchange(step)
        if step == 2:
            own_keys.start()
            own_values.start()
            get_angles.start()
    peak[...] = jnp.zeros_like(peak)
    gains[...] = jnp.broadcast_to(gain[...], gains.shape).T
    own_keys.wait()
    own_values.wait()
    get_angles.wait()
    for i in range(1, PARTS):
        source = (me + i) % PARTS
        pltpu.make_async_copy(held.at[source], held.at[source], key_came.at[source]).wait()

    @pl.loop(FIRST_TURN, STEPS)
    def _(step):
        for k in range(FIRST_TURN, STEPS):
            @pl.when(step == k)
            def _():
                exchange(k)

        @pl.when(step < FIRST_NARROW)
        def _():
            @pl.loop(0, TURNS)
            def _(i):
                turn((step - FIRST_TURN) * TURNS + i)

        @pl.when((step >= FIRST_NARROW) & (step < FIRST_NARROW + PARTS // NARROWS))
        def _():
            @pl.loop(0, NARROWS)
            def _(i):
                narrow((step - FIRST_NARROW) * NARROWS + i)

    out_scale[...] = jnp.max(peak[...].T, axis=0, keepdims=True)
    whole = pl.ds(0, PARTS)
    sends = sum(len(s) for s in COARSE_PLAN) + 2 * STEPS
    for _ in range(sends // PARTS):
        pltpu.make_async_copy(values.at[whole], values.at[whole], sent).wait()
    if sends % PARTS:
        rest = pl.ds(0, sends % PARTS)
        pltpu.make_async_copy(values.at[rest], values.at[rest], sent).wait()
    rest = pl.ds(0, PARTS - 1)
    pltpu.make_async_copy(values.at[rest], values.at[rest], value_came).wait()


def local(fresh_keys, fresh_values, turn_angle, key_gain):
    batch, block, _, size = fresh_keys.shape
    length = turn_angle.shape[0]
    hbm = pl.BlockSpec(memory_space=pltpu.HBM)
    vmem = pl.BlockSpec(memory_space=pltpu.VMEM)
    out_keys, out_values, out_scale = pl.pallas_call(
        kernel,
        name="exchange",
        out_shape=[
            pltpu.VMEM((size, length), jnp.bfloat16),
            pltpu.VMEM((batch, block, size), jnp.bfloat16),
            jax.ShapeDtypeStruct((1, size), jnp.float32),
        ],
        in_specs=[hbm, hbm, hbm, vmem],
        out_specs=[vmem, vmem, vmem],
        scratch_shapes=[
            pltpu.VMEM((batch, block, size), jnp.bfloat16),
            pltpu.VMEM((size, length), jnp.float32),
            pltpu.VMEM((size // 2, length), jnp.float32),
            pltpu.VMEM((size, CHUNK), jnp.float32),
            pltpu.VMEM((size, CHUNK), jnp.float32),
            pltpu.VMEM((SLOTS, block, size), jnp.bfloat16),
            pltpu.SemaphoreType.DMA,
            pltpu.SemaphoreType.DMA((SLOTS,)),
            pltpu.SemaphoreType.DMA((PARTS,)),
            pltpu.SemaphoreType.DMA,
            pltpu.SemaphoreType.DMA((3,)),
        ],
        compiler_params=pltpu.CompilerParams(
            collective_id=0, has_side_effects=True, vmem_limit_bytes=52 * 2**20
        ),
    )(
        fresh_keys.reshape(batch, block, size),
        fresh_values.reshape(batch, block, size),
        turn_angle.T,
        key_gain.reshape(1, size),
    )
    return (
        out_keys.reshape(1, 1, size, length),
        out_values.reshape(1, length, 1, size),
        out_scale.reshape(1, 1, size),
    )


def solution(mesh):
    in_specs = (
        P(None, ("coarse", "fine"), "group", None),
        P(None, ("coarse", "fine"), "group", None),
        P(),
        P(),
    )
    out_specs = (
        P(("coarse", "fine"), "group", None, None),
        P(("coarse", "fine"), None, "group", None),
        P(("coarse", "fine"), "group", None),
    )
    return jax.shard_map(local, mesh=mesh, in_specs=in_specs, out_specs=out_specs, check_vma=False)
```

time: 215 us -> 197 us (0.916)
  Pallas kernels: 0 us -> 192 us
  waiting for transfers between devices: 144 us -> 0 us
  other arithmetic: 26.4 us -> 0 us
  local copies, waits for them, and re-layouts: 27.7 us -> 4.54 us
  starting transfers between devices: 16.7 us -> 0 us
    pallas_call x0 -> x1, Pallas kernels: none -> 192 us  [local(): pl.pallas_call(kernel, name='exchange', out_shape=[pltpu.VMEM((size, leng...]
    all_to_all x2 -> x0, waiting for transfers between devices: 144 us -> none  [the longest x1 80.3 us: local(): lax.all_to_all(fresh_keys, ('coarse', 'fine'), split_axis=0, concat_axis=...]
    all_to_all x2 -> x0, starting transfers between devices: 16.7 us -> none  [the longest x1 11.6 us: local(): lax.all_to_all(fresh_keys, ('coarse', 'fine'), split_axis=0, concat_axis=...]
    cos x1 -> x0, local copies, waits for them, and re-layouts: 16.7 us -> none  [turn_pairs(): jnp.cos(angle)[None, :, None, :]]
    sub x1 -> x0, other arithmetic: 8.79 us -> none  [turn_pairs(): first * cosine - second * sine]
    mul x1 -> x0, other arithmetic: 7.55 us -> none  [root_norm(): vectors * lax.rsqrt(jnp.mean(vectors * vectors, axis=-1, keepdims=True) +...]
    convert_element_type x1 -> x0, local copies, waits for them, and re-layouts: 6.98 us -> none  [ready_to_store(): wide_keys = plain_keys.astype(jnp.float32)]
    reduce_sum x1 -> x0, other arithmetic: 4.45 us -> none  [root_norm(): jnp.mean(vectors * vectors, axis=-1, keepdims=True) + 1e-06]
  transfers between devices with their start and end apart: 2 -> 0, of which waited for: 2 -> 0; matrix products, arithmetic and copies ran while one was open for 23% -> 0% of each run, Pallas kernels for 0% -> 0%
where the time goes in v1:
time: 197 us
  Pallas kernels  192 us (97%)
  local copies, waits for them, and re-layouts  4.54 us (2%)
    pallas_call x1, Pallas kernels, local(): pl.pallas_call(kernel, name='exchange', out_shape=[pltpu.VMEM((size, leng...  192 us
    unnamed x5, local copies, waits for them, and re-layouts  4.54 us

profile of v1, /device:TPU:2, one launch (start us, length us, event | category | flops | bytes accessed | tf_op | source)
XLA Modules:
  0.0 197.3 jit_solution(14964788590787208666)
XLA Ops:
  0.6 192.1 %exchange.1 = (bf16[128,16384]{1,0:T(8,128)(2,1)S(1)}, bf16[32,512,128]{2,1,0:T(8,128)(2,1)S(1)}, f32[1,128]{1,0:T(1,128)}) custom-call(bf16[32,512,128]{2,1,0:T(8,128)(2,1)} %bitcast.9, bf16[32,512,128]{2,1,0:T(8,128)(2,1)} %bitcast.10, f32[64,16384]{1,0:T(8,128)} %bitcast.11, f32[1,128]{1,0:T(1,128)} %bitcast.12), custom_call_target="tpu_custom_call" | custom-call | tf_op jit(solution)/shard_map/exchange/pallas_call | solution.py:214
  192.8 2.0 %copy.10 = bf16[1,1,128,16384]{3,2,1,0:T(8,128)(2,1)} copy(bf16[1,1,128,16384]{3,2,1,0:T(8,128)(2,1)S(1)} %bitcast.8) | data formatting | bytes 8388608
  194.8 0.0 copy-start
  194.8 2.0 %copy.11 = bf16[1,16384,1,128]{3,1,2,0:T(8,128)(2,1)} copy(bf16[1,16384,1,128]{3,1,2,0:T(8,128)(2,1)S(1)} %bitcast.7) | data formatting | bytes 8388608
  196.8 0.0 copy-done
  196.8 0.5 copy.12
Async XLA Ops:
  194.8 2.0 %copy-start = (f32[1,128]{1,0:T(1,128)S(1)}, f32[1,128]{1,0:T(1,128)}, u32[]{:S(2)}) copy-start(f32[1,128]{1,0:T(1,128)} %get-tuple-element.8) | copy-start | bytes 1540

commit v2 on v1

--- a/solution.py
+++ b/solution.py
@@ -9,6 +9,8 @@
 COARSE, FINE = 4, 8
 PARTS = COARSE * FINE
 CHUNK = 128
+PIECES = 1
+EARLY = 1
 KEYS, VALUES = 0, 1
 LAG = 3
 AHEAD = 4
@@ -51,6 +53,7 @@
 COARSE_PLAN = coarse_plan()
 FINE_PLAN = {way: fine_plan(way) for way in (1, -1)}
 STEPS = len(FINE_PLAN[1])
+TWO_AWAY = next(j for j, step in enumerate(COARSE_PLAN) if step[0][1] == 2)
 SLOT = {}
 for _step in COARSE_PLAN:
     for _array, _rows, _off in _step:
@@ -60,6 +63,9 @@
     for _array, _hops, _rows, _done in FINE_PLAN[_way]:
         if _done:
             SLOT["passing", _way, _array, _hops, _rows, _done] = len(SLOT)
+for _way in FINE_PLAN:
+    for _array, _hops, _rows, _done in FINE_PLAN[_way][:EARLY]:
+        SLOT["early", _way, _array, _hops] = len(SLOT)
 SLOTS = len(SLOT)
 FIRST_TURN = STEPS // 2 + LAG + 1
 TURNS = 2
@@ -68,8 +74,8 @@
 
 
 def kernel(keys, values, angle, gain, out_keys, out_values, out_scale,
-           held, turned, angles, peak, gains, box,
-           sent, box_came, key_came, value_came, local_sem):
+           held, turned, angles, peak, gains, gain_row, box,
+           sent, box_came, key_came, value_came, local_sem, beyond):
     c, f, g = (lax.axis_index(name) for name in ("coarse", "fine", "group"))
     block = held.shape[1]
     me = c * FINE + f
@@ -79,11 +85,19 @@
     def at(row, column):
         return ((c + row) % COARSE, (f + column + FINE) % FINE, g)
 
-    near = [(0, 1), (0, -1), (1, 0), (3, 0), (2, 0)]
+    near = [(0, 1), (0, -1), (1, 0), (3, 0)]
     barrier = pltpu.get_barrier_semaphore()
     for row, column in near:
         pl.semaphore_signal(barrier, inc=1, device_id=at(row, column), device_id_type=MESH)
+    for way in FINE_PLAN:
+        for array, hops, _, _ in FINE_PLAN[way][:EARLY]:
+            slot = SLOT["early", way, array, hops]
+            off = hops if hops == FINE // 2 else way * hops
+            pltpu.make_async_copy(
+                source_of[array].at[c * FINE + (f + off + FINE) % FINE], box.at[slot], box_came.at[slot]
+            ).start()
     pl.semaphore_wait(barrier, len(near))
+    pl.semaphore_signal(beyond, inc=1, device_id=at(1, 0), device_id_type=MESH)
 
     def came(array, device):
         return key_came.at[device] if array == KEYS else value_came
@@ -107,7 +121,7 @@
         elif rows:
             slot = SLOT["staged", array, rows, off]
         else:
-            slot = None
+            slot = SLOT.get(("early", way, array, hops))
         if slot is None:
             source = source_of[array].at[c * FINE + (f + off + FINE) % FINE]
         else:
@@ -125,11 +139,16 @@
         ).start()
 
     def exchange(step):
+        for way in FINE_PLAN:
+            send_fine(way, *FINE_PLAN[way][step])
+        if step == 0:
+            for entry in sum(COARSE_PLAN[:AHEAD], []):
+                send_coarse(*entry)
+        if step + AHEAD == TWO_AWAY:
+            pl.semaphore_wait(beyond, 1)
         if step + AHEAD < len(COARSE_PLAN):
             for entry in COARSE_PLAN[step + AHEAD]:
                 send_coarse(*entry)
-        for way in FINE_PLAN:
-            send_fine(way, *FINE_PLAN[way][step])
 
     def turn(source):
         @pl.loop(0, block // CHUNK)
@@ -155,10 +174,9 @@
         scale = jnp.max(peak[...], axis=1, keepdims=True)
         out_keys[:, where] = (turned[:, where] / scale).astype(out_keys.dtype)
 
-    for entry in sum(COARSE_PLAN[:AHEAD], []):
-        send_coarse(*entry)
     own_keys = pltpu.make_async_copy(keys.at[me], held.at[me], local_sem.at[0])
     own_values = pltpu.make_async_copy(values.at[me], out_values.at[me], local_sem.at[1])
+    get_gain = pltpu.make_async_copy(gain, gain_row, local_sem.at[3])
     get_angles = pltpu.make_async_copy(angle, angles, local_sem.at[2])
     for step in range(FIRST_TURN):
         exchange(step)
@@ -166,8 +184,10 @@
             own_keys.start()
             own_values.start()
             get_angles.start()
+            get_gain.start()
     peak[...] = jnp.zeros_like(peak)
-    gains[...] = jnp.broadcast_to(gain[...], gains.shape).T
+    get_gain.wait()
+    gains[...] = jnp.broadcast_to(gain_row[...], gains.shape).T
     own_keys.wait()
     own_values.wait()
     get_angles.wait()
@@ -204,6 +224,21 @@
         pltpu.make_async_copy(values.at[rest], values.at[rest], sent).wait()
     rest = pl.ds(0, PARTS - 1)
     pltpu.make_async_copy(values.at[rest], values.at[rest], value_came).wait()
+
+
+def store(keys, values, scale, out_keys, out_values, out_scale, done):
+    copies = [pltpu.make_async_copy(scale, out_scale, done.at[0])]
+    for a, (held, out) in enumerate(((keys, out_keys), (values, out_values))):
+        rows = held.shape[0] // PIECES
+        for i in range(PIECES):
+            piece = pl.ds(i * rows, rows)
+            copies.append(
+                pltpu.make_async_copy(held.at[piece], out.at[piece], done.at[1 + a * PIECES + i])
+            )
+    for copy in copies:
+        copy.start()
+    for copy in copies:
+        copy.wait()
 
 
 def local(fresh_keys, fresh_values, turn_angle, key_gain):
@@ -217,9 +252,9 @@
         out_shape=[
             pltpu.VMEM((size, length), jnp.bfloat16),
             pltpu.VMEM((batch, block, size), jnp.bfloat16),
-            jax.ShapeDtypeStruct((1, size), jnp.float32),
+            pltpu.VMEM((1, size), jnp.float32),
         ],
-        in_specs=[hbm, hbm, hbm, vmem],
+        in_specs=[hbm, hbm, hbm, hbm],
         out_specs=[vmem, vmem, vmem],
         scratch_shapes=[
             pltpu.VMEM((batch, block, size), jnp.bfloat16),
@@ -227,12 +262,14 @@
             pltpu.VMEM((size // 2, length), jnp.float32),
             pltpu.VMEM((size, CHUNK), jnp.float32),
             pltpu.VMEM((size, CHUNK), jnp.float32),
+            pltpu.VMEM((1, size), jnp.float32),
             pltpu.VMEM((SLOTS, block, size), jnp.bfloat16),
             pltpu.SemaphoreType.DMA,
             pltpu.SemaphoreType.DMA((SLOTS,)),
             pltpu.SemaphoreType.DMA((PARTS,)),
             pltpu.SemaphoreType.DMA,
-            pltpu.SemaphoreType.DMA((3,)),
+            pltpu.SemaphoreType.DMA((4,)),
+            pltpu.SemaphoreType.REGULAR,
         ],
         compiler_params=pltpu.CompilerParams(
             collective_id=0, has_side_effects=True, vmem_limit_bytes=52 * 2**20
@@ -243,6 +280,19 @@
         turn_angle.T,
         key_gain.reshape(1, size),
     )
+    out_keys, out_values, out_scale = pl.pallas_call(
+        store,
+        name="store",
+        out_shape=[
+            jax.ShapeDtypeStruct((size, length), jnp.bfloat16),
+            jax.ShapeDtypeStruct((batch, block, size), jnp.bfloat16),
+            jax.ShapeDtypeStruct((1, size), jnp.float32),
+        ],
+        in_specs=[vmem, vmem, vmem],
+        out_specs=[hbm, hbm, hbm],
+        scratch_shapes=[pltpu.SemaphoreType.DMA((1 + 2 * PIECES,))],
+        compiler_params=pltpu.CompilerParams(vmem_limit_bytes=16 * 2**20),
+    )(out_keys, out_values, out_scale)
     return (
         out_keys.reshape(1, 1, size, length),
         out_values.reshape(1, length, 1, size),

time: 197 us -> 195 us (0.990)
  local copies, waits for them, and re-layouts: 4.54 us -> 0 us
  Pallas kernels: 192 us -> 194 us
    unnamed x5 -> x0, local copies, waits for them, and re-layouts: 4.54 us -> none
    pallas_call x0 -> x1, Pallas kernels: none -> 3.42 us  [local(): pl.pallas_call(store, name='store', out_shape=[jax.ShapeDtypeStruct((size...]
where the time goes in v2:
time: 195 us
  Pallas kernels  194 us (99%)
    pallas_call x1, Pallas kernels, local(): pl.pallas_call(kernel, name='exchange', out_shape=[pltpu.VMEM((size, leng...  191 us

profile of v2, /device:TPU:2, one launch (start us, length us, event | category | flops | bytes accessed | tf_op | source)
XLA Modules:
  0.0 194.7 jit_solution(16473413286899825607)
XLA Ops:
  0.6 190.6 %exchange.1 = (bf16[128,16384]{1,0:T(8,128)(2,1)S(1)}, bf16[32,512,128]{2,1,0:T(8,128)(2,1)S(1)}, f32[1,128]{1,0:T(1,128)S(1)}) custom-call(bf16[32,512,128]{2,1,0:T(8,128)(2,1)} %bitcast.7, bf16[32,512,128]{2,1,0:T(8,128)(2,1)} %bitcast.8, f32[64,16384]{1,0:T(8,128)} %bitcast.9, f32[1,128]{1,0:T(1,128)} %bitcast.10), custom_call_target="tpu_custom_call" | custom-call | tf_op jit(solution)/shard_map/exchange/pallas_call | solution.py:249
  191.3 3.4 %store.1 = (bf16[128,16384]{1,0:T(8,128)(2,1)}, bf16[32,512,128]{2,1,0:T(8,128)(2,1)}, f32[1,128]{1,0:T(1,128)}) custom-call(bf16[128,16384]{1,0:T(8,128)(2,1)S(1)} %get-tuple-element.9.keys, bf16[32,512,128]{2,1,0:T(8,128)(2,1)S(1)} %get-tuple-element.10.values, f32[1,128]{1,0:T(1,128)S(1)} %get-tuple-element.11.scale), custom_call_target="tpu_custom_call" | custom-call | tf_op jit(solution)/shard_map/store/pallas_call | solution.py:283

commit v3 on v2

--- a/solution.py
+++ b/solution.py
@@ -53,7 +53,6 @@
 COARSE_PLAN = coarse_plan()
 FINE_PLAN = {way: fine_plan(way) for way in (1, -1)}
 STEPS = len(FINE_PLAN[1])
-TWO_AWAY = next(j for j, step in enumerate(COARSE_PLAN) if step[0][1] == 2)
 SLOT = {}
 for _step in COARSE_PLAN:
     for _array, _rows, _off in _step:
@@ -85,10 +84,18 @@
     def at(row, column):
         return ((c + row) % COARSE, (f + column + FINE) % FINE, g)
 
-    near = [(0, 1), (0, -1), (1, 0), (3, 0)]
     barrier = pltpu.get_barrier_semaphore()
-    for row, column in near:
-        pl.semaphore_signal(barrier, inc=1, device_id=at(row, column), device_id_type=MESH)
+    last = COARSE - 1
+
+    def greet(semaphore, rows, column=0):
+        pl.semaphore_signal(
+            semaphore, inc=1, device_id=at(rows, column), device_id_type=MESH
+        )
+
+    greet(barrier, 0, 1)
+    greet(barrier, 0, -1)
+    pl.when(c > 0)(lambda: greet(barrier, last))
+    pl.when(c < last)(lambda: greet(barrier, 1))
     for way in FINE_PLAN:
         for array, hops, _, _ in FINE_PLAN[way][:EARLY]:
             slot = SLOT["early", way, array, hops]
@@ -96,8 +103,22 @@
             pltpu.make_async_copy(
                 source_of[array].at[c * FINE + (f + off + FINE) % FINE], box.at[slot], box_came.at[slot]
             ).start()
-    pl.semaphore_wait(barrier, len(near))
-    pl.semaphore_signal(beyond, inc=1, device_id=at(1, 0), device_id_type=MESH)
+    pl.semaphore_wait(barrier, 2 + (c + last) // COARSE + (2 * last - c) // COARSE)
+    inner = (c > 0) & (c < last)
+
+    @pl.when(inner)
+    def _():
+        greet(beyond, last)
+        greet(beyond, 1)
+
+    def greet_the_rest():
+        @pl.when(inner)
+        def _():
+            pl.semaphore_wait(beyond, 1)
+
+        pl.when(c == 1)(lambda: greet(beyond, last))
+        pl.when(c == last - 1)(lambda: greet(beyond, 1))
+        pl.when((c == 0) | (c == last))(lambda: pl.semaphore_wait(beyond, 2))
 
     def came(array, device):
         return key_came.at[device] if array == KEYS else value_came
@@ -141,11 +162,12 @@
     def exchange(step):
         for way in FINE_PLAN:
             send_fine(way, *FINE_PLAN[way][step])
-        if step == 0:
-            for entry in sum(COARSE_PLAN[:AHEAD], []):
+        if step < LAG - 1:
+            return
+        if step == LAG - 1:
+            greet_the_rest()
+            for entry in sum(COARSE_PLAN[: AHEAD + step], []):
                 send_coarse(*entry)
-        if step + AHEAD == TWO_AWAY:
-            pl.semaphore_wait(beyond, 1)
         if step + AHEAD < len(COARSE_PLAN):
             for entry in COARSE_PLAN[step + AHEAD]:
                 send_coarse(*entry)

time: 195 us -> 193 us (0.990)
  no operation moved by 1% of the time
where the time goes in v3:
time: 193 us
  Pallas kernels  193 us (100%)
    pallas_call x1, Pallas kernels, local(): pl.pallas_call(kernel, name='exchange', out_shape=[pltpu.VMEM((size, leng...  189 us

profile of v3, /device:TPU:2, one launch (start us, length us, event | category | flops | bytes accessed | tf_op | source)
XLA Modules:
  0.0 193.2 jit_solution(2848683524306773794)
XLA Ops:
  0.6 189.2 %exchange.1 = (bf16[128,16384]{1,0:T(8,128)(2,1)S(1)}, bf16[32,512,128]{2,1,0:T(8,128)(2,1)S(1)}, f32[1,128]{1,0:T(1,128)S(1)}) custom-call(bf16[32,512,128]{2,1,0:T(8,128)(2,1)} %bitcast.7, bf16[32,512,128]{2,1,0:T(8,128)(2,1)} %bitcast.8, f32[64,16384]{1,0:T(8,128)} %bitcast.9, f32[1,128]{1,0:T(1,128)} %bitcast.10), custom_call_target="tpu_custom_call" | custom-call | tf_op jit(solution)/shard_map/exchange/pallas_call | solution.py:271
  189.8 3.4 %store.1 = (bf16[128,16384]{1,0:T(8,128)(2,1)}, bf16[32,512,128]{2,1,0:T(8,128)(2,1)}, f32[1,128]{1,0:T(1,128)}) custom-call(bf16[128,16384]{1,0:T(8,128)(2,1)S(1)} %get-tuple-element.9.keys, bf16[32,512,128]{2,1,0:T(8,128)(2,1)S(1)} %get-tuple-element.10.values, f32[1,128]{1,0:T(1,128)S(1)} %get-tuple-element.11.scale), custom_call_target="tpu_custom_call" | custom-call | tf_op jit(solution)/shard_map/store/pallas_call | solution.py:305

commit v4 on v3

--- a/solution.py
+++ b/solution.py
@@ -65,7 +65,18 @@
 for _way in FINE_PLAN:
     for _array, _hops, _rows, _done in FINE_PLAN[_way][:EARLY]:
         SLOT["early", _way, _array, _hops] = len(SLOT)
+SPLIT = {1: (FORWARD4[VALUES][0], 4), -1: (0, 3)}
+for _way in SPLIT:
+    for _own in (True, False):
+        for _done in range(1, FINE // 2):
+            SLOT["half", _way, _own, _done] = len(SLOT)
 SLOTS = len(SLOT)
+HALF_SENDS = {
+    key: n
+    for n, key in enumerate(
+        (way, part, done) for way in SPLIT for part in range(3) for done in range(FINE // 2)
+    )
+}
 FIRST_TURN = STEPS // 2 + LAG + 1
 TURNS = 2
 FIRST_NARROW = FIRST_TURN + PARTS // TURNS
@@ -74,7 +85,7 @@
 
 def kernel(keys, values, angle, gain, out_keys, out_values, out_scale,
            held, turned, angles, peak, gains, gain_row, box,
-           sent, box_came, key_came, value_came, local_sem, beyond):
+           sent, half_sent, box_came, key_came, value_came, local_sem, beyond):
     c, f, g = (lax.axis_index(name) for name in ("coarse", "fine", "group"))
     block = held.shape[1]
     me = c * FINE + f
@@ -159,9 +170,60 @@
             device_id=at(0, way), device_id_type=MESH,
         ).start()
 
+    def half_send(way, part, done, act):
+        home_column = (f - way * done + FINE) % FINE
+        if part == 0:
+            act()
+        elif part == 1:
+            pl.when(home_column != SPLIT[way][1])(act)
+        else:
+            pl.when(home_column == SPLIT[-way][1])(act)
+
+    def send_split(way, done):
+        for part in range(3):
+            rows = SPLIT[way if part < 2 else -way][0]
+            piece = pl.ds(0 if part == 0 else block // 2, block // 2)
+
+            def act(part=part, rows=rows, piece=piece):
+                hops, array = FINE // 2, VALUES
+
+                def passing(at_hop):
+                    if part == 0:
+                        return SLOT["passing", way, array, hops, rows, at_hop]
+                    return SLOT["half", way, part == 1, at_hop]
+
+                if done:
+                    slot = passing(done)
+                    source = box.at[slot, piece]
+                    pltpu.make_async_copy(source, source, box_came.at[slot]).wait()
+                elif rows:
+                    slot = SLOT["staged", array, rows, hops]
+                    if part == 0:
+                        whole = box.at[slot]
+                        pltpu.make_async_copy(whole, whole, box_came.at[slot]).wait()
+                    source = box.at[slot, piece]
+                else:
+                    source = source_of[array].at[c * FINE + (f + hops) % FINE, piece]
+                if done + 1 < hops:
+                    slot = passing(done + 1)
+                    target, arrived = box.at[slot, piece], box_came.at[slot]
+                else:
+                    home = ((c + COARSE - rows) % COARSE) * FINE + (f - way * done + FINE) % FINE
+                    target, arrived = final_of[array].at[home, piece], value_came
+                pltpu.make_async_remote_copy(
+                    src_ref=source, dst_ref=target, send_sem=half_sent.at[HALF_SENDS[way, part, done]],
+                    recv_sem=arrived, device_id=at(0, way), device_id_type=MESH,
+                ).start()
+
+            half_send(way, part, done, act)
+
     def exchange(step):
         for way in FINE_PLAN:
-            send_fine(way, *FINE_PLAN[way][step])
+            array, hops, rows, done = FINE_PLAN[way][step]
+            if (array, hops, rows) == (VALUES, FINE // 2, SPLIT[way][0]):
+                send_split(way, done)
+            else:
+                send_fine(way, array, hops, rows, done)
         if step < LAG - 1:
             return
         if step == LAG - 1:
@@ -238,12 +300,17 @@
 
     out_scale[...] = jnp.max(peak[...].T, axis=0, keepdims=True)
     whole = pl.ds(0, PARTS)
-    sends = sum(len(s) for s in COARSE_PLAN) + 2 * STEPS
+    sends = sum(len(s) for s in COARSE_PLAN) + 2 * STEPS - 2 * (FINE // 2)
     for _ in range(sends // PARTS):
         pltpu.make_async_copy(values.at[whole], values.at[whole], sent).wait()
     if sends % PARTS:
         rest = pl.ds(0, sends % PARTS)
         pltpu.make_async_copy(values.at[rest], values.at[rest], sent).wait()
+    for (way, part, done), n in HALF_SENDS.items():
+        half = values.at[0, pl.ds(0, block // 2)]
+        half_send(
+            way, part, done, lambda n=n: pltpu.make_async_copy(half, half, half_sent.at[n]).wait()
+        )
     rest = pl.ds(0, PARTS - 1)
     pltpu.make_async_copy(values.at[rest], values.at[rest], value_came).wait()
 
@@ -287,6 +354,7 @@
             pltpu.VMEM((1, size), jnp.float32),
             pltpu.VMEM((SLOTS, block, size), jnp.bfloat16),
             pltpu.SemaphoreType.DMA,
+            pltpu.SemaphoreType.DMA((len(HALF_SENDS),)),
             pltpu.SemaphoreType.DMA((SLOTS,)),
             pltpu.SemaphoreType.DMA((PARTS,)),
             pltpu.SemaphoreType.DMA,

time: 193 us -> 192 us (level)
  no operation moved by 1% of the time
where the time goes in v4:
time: 192 us
  Pallas kernels  192 us (100%)
    pallas_call x1, Pallas kernels, local(): pl.pallas_call(kernel, name='exchange', out_shape=[pltpu.VMEM((size, leng...  188 us

profile of v4, /device:TPU:2, one launch (start us, length us, event | category | flops | bytes accessed | tf_op | source)
XLA Modules:
  0.0 192.2 jit_solution(8268533303375502862)
XLA Ops:
  0.6 188.1 %exchange.1 = (bf16[128,16384]{1,0:T(8,128)(2,1)S(1)}, bf16[32,512,128]{2,1,0:T(8,128)(2,1)S(1)}, f32[1,128]{1,0:T(1,128)S(1)}) custom-call(bf16[32,512,128]{2,1,0:T(8,128)(2,1)} %bitcast.7, bf16[32,512,128]{2,1,0:T(8,128)(2,1)} %bitcast.8, f32[64,16384]{1,0:T(8,128)} %bitcast.9, f32[1,128]{1,0:T(1,128)} %bitcast.10), custom_call_target="tpu_custom_call" | custom-call | tf_op jit(solution)/shard_map/exchange/pallas_call | solution.py:338
  188.7 3.4 %store.1 = (bf16[128,16384]{1,0:T(8,128)(2,1)}, bf16[32,512,128]{2,1,0:T(8,128)(2,1)}, f32[1,128]{1,0:T(1,128)}) custom-call(bf16[128,16384]{1,0:T(8,128)(2,1)S(1)} %get-tuple-element.9.keys, bf16[32,512,128]{2,1,0:T(8,128)(2,1)S(1)} %get-tuple-element.10.values, f32[1,128]{1,0:T(1,128)S(1)} %get-tuple-element.11.scale), custom_call_target="tpu_custom_call" | custom-call | tf_op jit(solution)/shard_map/store/pallas_call | solution.py:373

commit v5 on v4

--- a/solution.py
+++ b/solution.py
@@ -85,7 +85,7 @@
 
 def kernel(keys, values, angle, gain, out_keys, out_values, out_scale,
            held, turned, angles, peak, gains, gain_row, box,
-           sent, half_sent, box_came, key_came, value_came, local_sem, beyond):
+           sent, half_sent, box_came, key_came, value_came, local_sem, beyond, ready):
     c, f, g = (lax.axis_index(name) for name in ("coarse", "fine", "group"))
     block = held.shape[1]
     me = c * FINE + f
@@ -96,16 +96,15 @@
         return ((c + row) % COARSE, (f + column + FINE) % FINE, g)
 
     barrier = pltpu.get_barrier_semaphore()
-    last = COARSE - 1
+    last, end = COARSE - 1, FINE - 1
 
     def greet(semaphore, rows, column=0):
         pl.semaphore_signal(
             semaphore, inc=1, device_id=at(rows, column), device_id_type=MESH
         )
 
-    greet(barrier, 0, 1)
-    greet(barrier, 0, -1)
-    pl.when(c > 0)(lambda: greet(barrier, last))
+    pl.when(f < end - 1)(lambda: greet(barrier, 0, 1))
+    pl.when((f == 0) | (f == end))(lambda: greet(barrier, 0, -1))
     pl.when(c < last)(lambda: greet(barrier, 1))
     for way in FINE_PLAN:
         for array, hops, _, _ in FINE_PLAN[way][:EARLY]:
@@ -114,17 +113,20 @@
             pltpu.make_async_copy(
                 source_of[array].at[c * FINE + (f + off + FINE) % FINE], box.at[slot], box_came.at[slot]
             ).start()
-    pl.semaphore_wait(barrier, 2 + (c + last) // COARSE + (2 * last - c) // COARSE)
+    heard = (f + end) // FINE + f // (end - 1) - f // end + (c + last) // COARSE
+    pl.when((f > 0) | (c > 0))(lambda: pl.semaphore_wait(barrier, heard))
+    pl.when((f > 0) & (f < end))(lambda: greet(ready.at[0], 0, -1))
+    pl.when(f >= end - 1)(lambda: greet(ready.at[1], 0, 1))
+    pl.when(c > 0)(lambda: greet(ready.at[2], last))
     inner = (c > 0) & (c < last)
 
-    @pl.when(inner)
-    def _():
-        greet(beyond, last)
-        greet(beyond, 1)
-
     def greet_the_rest():
+        pl.when(c < last)(lambda: pl.semaphore_wait(ready.at[2], 1))
+
         @pl.when(inner)
         def _():
+            greet(beyond, last)
+            greet(beyond, 1)
             pl.semaphore_wait(beyond, 1)
 
         pl.when(c == 1)(lambda: greet(beyond, last))
@@ -224,12 +226,6 @@
                 send_split(way, done)
             else:
                 send_fine(way, array, hops, rows, done)
-        if step < LAG - 1:
-            return
-        if step == LAG - 1:
-            greet_the_rest()
-            for entry in sum(COARSE_PLAN[: AHEAD + step], []):
-                send_coarse(*entry)
         if step + AHEAD < len(COARSE_PLAN):
             for entry in COARSE_PLAN[step + AHEAD]:
                 send_coarse(*entry)
@@ -258,17 +254,32 @@
         scale = jnp.max(peak[...], axis=1, keepdims=True)
         out_keys[:, where] = (turned[:, where] / scale).astype(out_keys.dtype)
 
+    def first_sends(way):
+        for step in range(LAG):
+            send_fine(way, *FINE_PLAN[way][step])
+
+    pl.when((f > 0) & (f < end))(lambda: first_sends(-1))
+    pl.when(f < end - 1)(lambda: pl.semaphore_wait(ready.at[0], 1))
+    first_sends(1)
+
+    @pl.when((f == 0) | (f == end))
+    def _():
+        pl.semaphore_wait(ready.at[1], 1)
+        first_sends(-1)
+
+    greet_the_rest()
+    for entry in sum(COARSE_PLAN[: AHEAD + LAG], []):
+        send_coarse(*entry)
     own_keys = pltpu.make_async_copy(keys.at[me], held.at[me], local_sem.at[0])
     own_values = pltpu.make_async_copy(values.at[me], out_values.at[me], local_sem.at[1])
     get_gain = pltpu.make_async_copy(gain, gain_row, local_sem.at[3])
     get_angles = pltpu.make_async_copy(angle, angles, local_sem.at[2])
-    for step in range(FIRST_TURN):
+    own_keys.start()
+    own_values.start()
+    get_angles.start()
+    get_gain.start()
+    for step in range(LAG, FIRST_TURN):
         exchange(step)
-        if step == 2:
-            own_keys.start()
-            own_values.start()
-            get_angles.start()
-            get_gain.start()
     peak[...] = jnp.zeros_like(peak)
     get_gain.wait()
     gains[...] = jnp.broadcast_to(gain_row[...], gains.shape).T
@@ -360,6 +371,7 @@
             pltpu.SemaphoreType.DMA,
             pltpu.SemaphoreType.DMA((4,)),
             pltpu.SemaphoreType.REGULAR,
+            pltpu.SemaphoreType.REGULAR((3,)),
         ],
         compiler_params=pltpu.CompilerParams(
             collective_id=0, has_side_effects=True, vmem_limit_bytes=52 * 2**20

time: 192 us -> 192 us (level)
  no operation moved by 1% of the time
where the time goes in v5:
time: 192 us
  Pallas kernels  191 us (99%)
    pallas_call x1, Pallas kernels, local(): pl.pallas_call(kernel, name='exchange', out_shape=[pltpu.VMEM((size, leng...  188 us

profile of v5, /device:TPU:2, one launch (start us, length us, event | category | flops | bytes accessed | tf_op | source)
XLA Modules:
  0.0 191.8 jit_solution(17259428361743149102)
XLA Ops:
  0.6 187.7 %exchange.1 = (bf16[128,16384]{1,0:T(8,128)(2,1)S(1)}, bf16[32,512,128]{2,1,0:T(8,128)(2,1)S(1)}, f32[1,128]{1,0:T(1,128)S(1)}) custom-call(bf16[32,512,128]{2,1,0:T(8,128)(2,1)} %bitcast.7, bf16[32,512,128]{2,1,0:T(8,128)(2,1)} %bitcast.8, f32[64,16384]{1,0:T(8,128)} %bitcast.9, f32[1,128]{1,0:T(1,128)} %bitcast.10), custom_call_target="tpu_custom_call" | custom-call | tf_op jit(solution)/shard_map/exchange/pallas_call | solution.py:349
  188.4 3.4 %store.1 = (bf16[128,16384]{1,0:T(8,128)(2,1)}, bf16[32,512,128]{2,1,0:T(8,128)(2,1)}, f32[1,128]{1,0:T(1,128)}) custom-call(bf16[128,16384]{1,0:T(8,128)(2,1)S(1)} %get-tuple-element.9.keys, bf16[32,512,128]{2,1,0:T(8,128)(2,1)S(1)} %get-tuple-element.10.values, f32[1,128]{1,0:T(1,128)S(1)} %get-tuple-element.11.scale), custom_call_target="tpu_custom_call" | custom-call | tf_op jit(solution)/shard_map/store/pallas_call | solution.py:385

commit v6 on v5

--- a/solution.py
+++ b/solution.py
@@ -9,7 +9,7 @@
 COARSE, FINE = 4, 8
 PARTS = COARSE * FINE
 CHUNK = 128
-PIECES = 1
+PIECES = 2
 EARLY = 1
 KEYS, VALUES = 0, 1
 LAG = 3
@@ -335,8 +335,8 @@
             copies.append(
                 pltpu.make_async_copy(held.at[piece], out.at[piece], done.at[1 + a * PIECES + i])
             )
-    for copy in copies:
-        copy.start()
+    for i, copy in enumerate(copies):
+        copy.start(priority=i % 2)
     for copy in copies:
         copy.wait()
 

time: 192 us -> 192 us (level)
  no operation moved by 1% of the time
where the time goes in v6:
time: 192 us
  Pallas kernels  191 us (99%)
    pallas_call x1, Pallas kernels, local(): pl.pallas_call(kernel, name='exchange', out_shape=[pltpu.VMEM((size, leng...  188 us

profile of v6, /device:TPU:2, one launch (start us, length us, event | category | flops | bytes accessed | tf_op | source)
XLA Modules:
  0.0 191.7 jit_solution(16429417452321356360)
XLA Ops:
  0.6 187.7 %exchange.1 = (bf16[128,16384]{1,0:T(8,128)(2,1)S(1)}, bf16[32,512,128]{2,1,0:T(8,128)(2,1)S(1)}, f32[1,128]{1,0:T(1,128)S(1)}) custom-call(bf16[32,512,128]{2,1,0:T(8,128)(2,1)} %bitcast.7, bf16[32,512,128]{2,1,0:T(8,128)(2,1)} %bitcast.8, f32[64,16384]{1,0:T(8,128)} %bitcast.9, f32[1,128]{1,0:T(1,128)} %bitcast.10), custom_call_target="tpu_custom_call" | custom-call | tf_op jit(solution)/shard_map/exchange/pallas_call | solution.py:349
  188.4 3.4 %store.1 = (bf16[128,16384]{1,0:T(8,128)(2,1)}, bf16[32,512,128]{2,1,0:T(8,128)(2,1)}, f32[1,128]{1,0:T(1,128)}) custom-call(bf16[128,16384]{1,0:T(8,128)(2,1)S(1)} %get-tuple-element.9.keys, bf16[32,512,128]{2,1,0:T(8,128)(2,1)S(1)} %get-tuple-element.10.values, f32[1,128]{1,0:T(1,128)S(1)} %get-tuple-element.11.scale), custom_call_target="tpu_custom_call" | custom-call | tf_op jit(solution)/shard_map/store/pallas_call | solution.py:385
